TPU v7x, 32 devices: a whole 2x2x4 slice. The times are simulated.
32 devices in a mesh: dp: 8 (over z, x), expert: 4 (over y, core).
Axes of the slice: x: 2, y: 2, z: 4, core: 2. Of those that a mesh axis runs over, the one named last changes fastest.
Arguments:
- tokens: bfloat16 [4096, 2048], P(('dp', 'expert')), may hold values from -6 to 6
- out_grad: bfloat16 [4096, 2048], P(('dp', 'expert')), may hold values from -3 to 3
- z_weight: float32 [4096], P(('dp', 'expert')), may hold values from 0.1 to 1
- router_weight: bfloat16 [2048, 128], replicated, may hold values from -0.125 to 0.125
- expert_ids: int32 [4096, 4], P(('dp', 'expert')), may hold values from 0 to 127, as said below
- gate_up_weight: bfloat16 [4, 2048, 3072], P('expert'), may hold values from -0.125 to 0.125
- down_weight: bfloat16 [4, 1536, 2048], P('expert'), may hold values from -0.15625 to 0.15625
Outputs:
- token_grad: bfloat16 [4096, 2048], P(('dp', 'expert'))
- router_grad: float32 [2048, 128], replicated
- gate_up_grad: bfloat16 [4, 2048, 3072], P('expert', 'dp')
- down_grad: bfloat16 [4, 1536, 2048], P('expert', 'dp')
Inputs may be any that keep to these rules, and one draw needn't show every extreme that they name: `expert_ids`: each row names 4 different experts. Experts 0 to 3 are the ones in flight. The 128 rows of one device name any one expert in flight at most 64 times; in every data group some expert in flight is named exactly 64 times by the rows of each device of the group.
All inputs are finite; a program needn't handle non-finite values.
Results may differ from a plain program's by a relative error of at most 0.019.
Values may be sent and summed in bfloat16 or wider, within the bound.
A program may use at most 192 MiB of HBM per device.

v0:
```python
import jax
import jax.numpy as jnp
from jax import lax
from jax.sharding import PartitionSpec as P


def expert_rows(rows_in, rows_grad, w_gateup, w_down, acc_gateup, acc_down):
    hidden_units = w_down.shape[0]
    pre_act = jnp.dot(rows_in, w_gateup, preferred_element_type=jnp.float32)
    gate_pre = pre_act[:, :hidden_units]
    up_pre = pre_act[:, hidden_units:]
    activated = jax.nn.silu(gate_pre)
    hidden = (activated * up_pre).astype(jnp.bfloat16)
    expert_out = jnp.dot(hidden, w_down, preferred_element_type=jnp.float32).astype(jnp.bfloat16)
    hidden_grad = lax.dot_general(
        rows_grad, w_down, (((1,), (1,)), ((), ())), preferred_element_type=jnp.float32
    )
    acc_down = lax.dot_general(
        hidden, rows_grad, (((0,), (0,)), ((), ())), preferred_element_type=jnp.float32
    )
    sigmoid_gate = jax.nn.sigmoid(gate_pre)
    gate_grad = hidden_grad * up_pre * sigmoid_gate * (1.0 + gate_pre * (1.0 - sigmoid_gate))
    up_grad = hidden_grad * activated
    pre_grad = jnp.concatenate([gate_grad, up_grad], axis=1).astype(jnp.bfloat16)
    acc_gateup = lax.dot_general(
        rows_in, pre_grad, (((0,), (0,)), ((), ())), preferred_element_type=jnp.float32
    )
    input_grad = lax.dot_general(
        pre_grad, w_gateup, (((1,), (1,)), ((), ())), preferred_element_type=jnp.float32
    ).astype(jnp.bfloat16)
    return (acc_gateup, acc_down, expert_out, input_grad)


def split_pair(values):
    upper = values.astype(jnp.bfloat16)
    lower = (values - upper.astype(jnp.float32)).astype(jnp.bfloat16)
    return jnp.stack([upper, lower], axis=-1)


def join_pair(pair):
    return pair[..., 0].astype(jnp.float32) + pair[..., 1].astype(jnp.float32)


def per_device(tokens, out_grad, z_weight, router_weight, expert_ids, gate_up_weight, down_weight):
    tok_count, width = tokens.shape
    top_count = expert_ids.shape[1]
    routed = router_weight.shape[1]
    flight = lax.axis_size("expert")
    capacity = tok_count // 2
    w_gateup = gate_up_weight[0]
    w_down = down_weight[0]
    hidden_units = w_down.shape[0]
    logits = jnp.dot(tokens, router_weight, preferred_element_type=jnp.float32)
    choose = expert_ids[:, :, None] == jnp.arange(routed, dtype=jnp.int32)[None, None, :]
    selected = jnp.sum(jnp.where(choose, logits[:, None, :], 0.0), axis=2)
    sel_exp = jnp.exp(selected)
    probs = sel_exp / jnp.sum(sel_exp, axis=1, keepdims=True)
    log_total = jnp.log(jnp.sum(jnp.exp(logits), axis=1))
    flat_ids = expert_ids.reshape(-1)
    slot_count = tok_count * top_count
    member = (flat_ids[:, None] == jnp.arange(flight, dtype=jnp.int32)[None, :]).astype(jnp.int32)
    ranks = jnp.sum((jnp.cumsum(member, axis=0) - 1) * member, axis=1)
    in_flight = flat_ids < flight
    position = jnp.where(in_flight, flat_ids * capacity + ranks, flight * capacity)
    source_slot = (
        jnp.zeros((flight * capacity,), jnp.int32)
        .at[position]
        .set(jnp.arange(slot_count, dtype=jnp.int32), mode="drop")
    )
    filled = jnp.zeros((flight * capacity,), jnp.bool_).at[position].set(True, mode="drop")
    source_tok = source_slot // top_count
    send_in = jnp.where(filled[:, None], tokens[source_tok], 0)
    slot_prob = jnp.where(filled, probs.reshape(-1)[source_slot], 0.0)
    counts = jnp.sum(member, axis=0)
    count_msg = jnp.stack([counts // 128, counts % 128], axis=1).astype(jnp.bfloat16)
    send_raw = jnp.where(filled[:, None], out_grad[source_tok], 0)
    prob_pair = split_pair(slot_prob)
    recv_in, recv_raw, recv_prob, recv_counts = (
        lax.all_to_all(
            send_in.reshape(flight, capacity, width),
            "expert",
            split_axis=0,
            concat_axis=0,
            tiled=True,
        ),
        lax.all_to_all(
            send_raw.reshape(flight, capacity, width),
            "expert",
            split_axis=0,
            concat_axis=0,
            tiled=True,
        ),
        lax.all_to_all(
            prob_pair.reshape(flight, capacity, 2),
            "expert",
            split_axis=0,
            concat_axis=0,
            tiled=True,
        ),
        lax.all_to_all(count_msg, "expert", split_axis=0, concat_axis=0, tiled=True),
    )
    sources = recv_in.shape[0]
    total_rows = sources * capacity
    flat_in = recv_in.reshape(total_rows, width)
    flat_raw = recv_raw.reshape(total_rows, width)
    row_prob = join_pair(recv_prob.reshape(total_rows, 2))
    flat_grad = (row_prob[:, None] * flat_raw.astype(jnp.float32)).astype(jnp.bfloat16)
    acc_gateup, acc_down, produced, back_rows = expert_rows(
        flat_in,
        flat_grad,
        w_gateup,
        w_down,
        jnp.zeros((width, 2 * hidden_units), jnp.float32),
        jnp.zeros((hidden_units, width), jnp.float32),
    )
    slot_at = jnp.where(in_flight, position, 0)
    row_score = jnp.sum(flat_raw.astype(jnp.float32) * produced.astype(jnp.float32), axis=1)
    score_pair = split_pair(row_score)
    home_dx, home_pair = (
        lax.all_to_all(
            back_rows.reshape(sources, capacity, width),
            "expert",
            split_axis=0,
            concat_axis=0,
            tiled=True,
        ),
        lax.all_to_all(
            score_pair.reshape(sources, capacity, 2),
            "expert",
            split_axis=0,
            concat_axis=0,
            tiled=True,
        ),
    )
    flat_dx = home_dx.reshape(flight * capacity, width)
    flat_score = join_pair(home_pair.reshape(flight * capacity, 2))
    scores = jnp.where(in_flight, flat_score[slot_at], 0.0).reshape(tok_count, top_count)
    slot_dx = jnp.where(in_flight[:, None], flat_dx[slot_at], 0).reshape(
        tok_count, top_count, width
    )
    mean_score = jnp.sum(probs * scores, axis=1, keepdims=True)
    sel_grad = probs * (scores - mean_score)
    z_grad = 2.0 * z_weight[:, None] * log_total[:, None] * jnp.exp(logits - log_total[:, None])
    logit_grad = (z_grad + jnp.sum(jnp.where(choose, sel_grad[:, :, None], 0.0), axis=1)).astype(
        jnp.bfloat16
    )
    token_grad = (
        jnp.sum(slot_dx.astype(jnp.float32), axis=1)
        + lax.dot_general(
            logit_grad, router_weight, (((1,), (1,)), ((), ())), preferred_element_type=jnp.float32
        )
    ).astype(jnp.bfloat16)
    router_part = lax.dot_general(
        tokens, logit_grad, (((0,), (0,)), ((), ())), preferred_element_type=jnp.float32
    )
    router_grad = lax.psum(router_part, ("dp", "expert"))
    part_gateup = acc_gateup.astype(jnp.bfloat16)
    part_down = acc_down.astype(jnp.bfloat16)
    gate_up_grad, down_grad = (
        lax.psum_scatter(part_gateup[None], "dp", scatter_dimension=1, tiled=True).astype(
            jnp.float32
        ),
        lax.psum_scatter(part_down[None], "dp", scatter_dimension=1, tiled=True).astype(
            jnp.float32
        ),
    )
    return (
        token_grad,
        router_grad,
        gate_up_grad.astype(jnp.bfloat16),
        down_grad.astype(jnp.bfloat16),
    )


def solution(mesh):
    return jax.shard_map(
        per_device,
        mesh=mesh,
        in_specs=(
            P(("dp", "expert"), None),
            P(("dp", "expert"), None),
            P(("dp", "expert")),
            P(),
            P(("dp", "expert"), None),
            P("expert", None, None),
            P("expert", None, None),
        ),
        out_specs=(
            P(("dp", "expert"), None),
            P(),
            P("expert", "dp", None),
            P("expert", "dp", None),
        ),
        check_vma=False,
    )
```

profile of v0, /device:TPU:0, one launch (start us, length us, event | category | flops | bytes accessed | tf_op | source)
XLA Modules:
  0.0 440.1 jit_solution(1820209398362379599)
XLA Ops:
  8.0 0.7 broadcast_compare_fusion
  8.8 0.7 broadcast_multiply_fusion
  9.4 0.8 copy.45
  10.3 0.1 eq.38
  10.4 0.1 copy.42
  10.6 0.6 copy-done.5
  11.2 0.1 lt.55
  11.3 0.1 copy.44
  11.4 0.1 mul.92
  11.5 1.2 reduce-window.6
  12.8 0.2 slice_reduce_fusion
  13.0 0.2 reduce-window.9
  13.3 2.4 scatter_custom_fusion.1
  15.8 2.4 scatter_custom_fusion
  18.3 0.6 pad_clamp_fusion.1
  18.9 1.4 gather_fusion.2
  20.3 1.4 gather_fusion.1
  21.7 1.5 broadcast_select_fusion
  23.2 4.4 all-to-all-start.2
  27.6 0.4 exponential_reduce_fusion
  28.1 0.2 select_reduce_fusion.1
  28.3 0.6 multiply_multiply_fusion
  29.0 13.1 %all-to-all-done.2 = bf16[4,64,2048]{2,1,0:T(8,128)(2,1)S(1)} async-done(((bf16[4,64,2048]{2,1,0:T(8,128)(2,1)}), bf16[4,64,2048]{2,1,0:T(8,128)(2,1)S(1)}, u32[]{:S(2)}, u32[]{:S(2)}) %all-to-all-start.2) | async-done | bytes 1048608 | tf_op jit(solution)/shard_map/all_to_all | solution.py:79
  42.0 3.5 all-to-all-start.1
  45.6 9.7 %fusion.2 = f32[256,3072]{1,0:T(8,128)} fusion(bf16[256,2048]{1,0:T(8,128)(2,1)S(1)} %bitcast.81, bf16[1,2048,3072]{2,1,0:T(8,128)(2,1)} %param.12), kind=kOutput, calls=%fused_computation.9 | convolution fusion | flops 3221225472 | bytes 16777216 | tf_op jit(solution)/shard_map/dot_general | solution.py:9
  55.2 2.3 multiply_convert_fusion.1
  57.6 2.4 all-to-all-done.1
  60.0 4.8 %fusion.24 = f32[256]{0:T(256)S(1)} fusion(bf16[256,1536]{1,0:T(8,128)(2,1)S(1)} %multiply_convert_fusion.1, bf16[1,1536,2048]{2,1,0:T(8,128)(2,1)} %param.13, bf16[256,2048]{1,0:T(8,128)(2,1)S(1)} %bitcast.80), kind=kOutput, calls=%fused_computation.35 | convolution fusion | flops 1613233920 | bytes 8127488 | tf_op jit(solution)/shard_map/dot_general | solution.py:14
  64.8 0.6 copy.51
  65.4 3.4 all-to-all-start.4
  68.8 0.5 exponential_reduce_fusion.1
  69.4 3.0 all-to-all-done.4
  72.4 3.5 gather_fusion.4
  76.1 1.2 multiply_reduce_fusion
  77.3 0.6 copy-done.8
  77.9 0.1 copy.48
  78.0 0.1 div.31
  78.1 2.1 gather_fusion
  80.2 0.6 subtract_convert_fusion.1
  80.8 0.6 select_convert_fusion
  81.4 0.7 subtract_multiply_fusion
  82.2 0.6 copy.49
  82.8 3.2 all-to-all-start
  86.1 0.2 select_reduce_fusion
  86.3 0.7 copy.54
  87.0 0.9 add_convert_fusion
  87.9 1.3 convolution_bitcast_fusion
  89.2 0.5 all-to-all-done
  89.8 0.5 broadcast.186
  90.3 0.7 fusion.38
  91.0 0.2 fusion.22
  91.2 4.4 %fusion.4 = bf16[1,1536,2048]{2,1,0:T(8,128)(2,1)} fusion(bf16[256,1536]{1,0:T(8,128)(2,1)S(1)} %multiply_convert_fusion.1, bf16[256,2048]{1,0:T(8,128)(2,1)S(1)} %fusion.22), kind=kOutput, calls=%fused_computation.13 | convolution fusion | flops 1613758464 | bytes 8126464 | tf_op jit(solution)/shard_map/dot_general | solution.py:18
  95.8 0.2 multiply_convert_fusion
  96.1 6.0 %multiply_convert_fusion.3 = (bf16[256,1536]{1,0:T(8,128)(2,1)S(1)}, bf16[256,1536]{1,0:T(8,128)(2,1)S(1)}) fusion(f32[256,3072]{1,0:T(8,128)} %fusion.2, bf16[256,2048]{1,0:T(8,128)(2,1)S(1)} %bitcast.85, bf16[1,1536,2048]{2,1,0:T(8,128)(2,1)} %param.13), kind=kOutput, calls=%fused_computation.32 | convolution fusion | flops 1615724544 | bytes 12058624 | tf_op jit(solution)/shard_map/dot_general | solution.py:15
  102.1 6.6 %convert_bitcast_fusion = bf16[1,2048,3072]{2,1,0:T(8,128)(2,1)} fusion(bf16[256,2048]{1,0:T(8,128)(2,1)S(1)} %bitcast.82, bf16[256,1536]{1,0:T(8,128)(2,1)S(1)} %get-tuple-element.31, bf16[256,1536]{1,0:T(8,128)(2,1)S(1)} %get-tuple-element.30), kind=kOutput, calls=%fused_computation.11 | convolution fusion | flops 3230662656 | bytes 15204352 | tf_op jit(solution)/shard_map/dot_general | solution.py:25
  108.7 9.0 %fusion.18 = bf16[256,2048]{1,0:T(8,128)(2,1)} fusion(bf16[1,2048,3072]{2,1,0:T(8,128)(2,1)} %param.12, bf16[256,1536]{1,0:T(8,128)(2,1)S(1)} %get-tuple-element.31, bf16[256,1536]{1,0:T(8,128)(2,1)S(1)} %get-tuple-element.30), kind=kOutput, calls=%fused_computation.22 | convolution fusion | flops 3224895488 | bytes 15204352 | tf_op jit(solution)/shard_map/dot_general | solution.py:28
  117.8 3.9 all-to-all-start.3
  121.7 229.6 %all-reduce.2.cloned.1.call-done = f32[2048,128]{0,1:T(8,128)} async-done(((f32[2048,128]{0,1:T(8,128)}), f32[2048,128]{0,1:T(8,128)}) %all-reduce.2.cloned.1.call-update) | async-done | bytes 1048592 | tf_op jit(solution)/shard_map/psum | solution.py:156
  351.2 2.6 copy.55
  353.8 2.5 gather_fusion.3
  356.3 2.2 gather.29
  358.6 5.6 %convert_reduce_fusion = f32[128,2048]{1,0:T(8,128)S(1)} fusion(bf16[128,4,2048]{2,1,0:T(4,128)(2,1)} %gather.29, pred[128,4]{1,0:T(8,128)(4,1)S(1)} %copy-done.6), kind=kLoop, calls=%fused_computation.18 | loop fusion | flops 2883584 | bytes 3146240 | tf_op jit(solution)/shard_map/reduce_sum | solution.py:148
  364.1 1.1 fusion.21
  365.3 67.3 %reduce-scatter.3.cloned.1.call-done = bf16[1,256,3072]{2,1,0:T(8,128)(2,1)} async-done(((bf16[1,2048,3072]{2,1,0:T(8,128)(2,1)}), bf16[1,256,3072]{2,1,0:T(8,128)(2,1)}) %reduce-scatter.3.cloned.1.call-update) | async-done | bytes 1572880 | tf_op jit(solution)/shard_map/reduce_scatter | solution.py:160
  (57 shorter events, 1.4 us)
Async XLA Ops:
  8.0 10.9 %copy-start = (bf16[128,2048]{1,0:T(8,128)(2,1)S(1)}, bf16[128,2048]{1,0:T(8,128)(2,1)}, u32[]{:S(2)}) copy-start(bf16[128,2048]{1,0:T(8,128)(2,1)} %param.7) | copy-start | bytes 1572868
  10.6 0.6 copy-start.5
  18.2 0.7 copy-start.11
  18.9 1.4 copy-start.2
  23.2 4.4 %copy-start.3 = (bf16[2048,128]{1,0:T(8,128)(2,1)S(1)}, bf16[2048,128]{1,0:T(8,128)(2,1)}, u32[]{:S(2)}) copy-start(bf16[2048,128]{1,0:T(8,128)(2,1)} %param.10) | copy-start | bytes 1572868
  23.2 4.9 %copy-start.7 = (s32[128,4]{0,1:T(4,128)S(1)}, s32[128,4]{0,1:T(4,128)}, u32[]{:S(2)}) copy-start(s32[128,4]{0,1:T(4,128)} %param.11) | copy-start | bytes 6148
  23.2 5.1 %copy-start.12 = (f32[128]{0:T(128)S(1)}, f32[128]{0:T(128)}, u32[]{:S(2)}) copy-start(f32[128]{0:T(128)} %param.9) | copy-start | bytes 1540
  23.2 18.8 %all-to-all-start.2 = ((bf16[4,64,2048]{2,1,0:T(8,128)(2,1)}), bf16[4,64,2048]{2,1,0:T(8,128)(2,1)S(1)}, u32[]{:S(2)}, u32[]{:S(2)}) async-start(bf16[4,64,2048]{2,1,0:T(8,128)(2,1)} %get-tuple-element.38), calls=%async_computation.2 | async-start | bytes 2097152 | tf_op jit(solution)/shard_map/all_to_all | solution.py:79
  28.1 44.3 %copy-start.9 = (s32[1024]{0:T(1024)}, s32[1024]{0:T(1024)S(1)}, u32[]{:S(2)}) copy-start(s32[1024]{0:T(1024)S(1)} %pad_clamp_fusion) | copy-start | bytes 12292
  42.0 17.9 %all-to-all-start.1 = ((bf16[4,64,2048]{2,1,0:T(8,128)(2,1)}), bf16[4,64,2048]{2,1,0:T(8,128)(2,1)S(1)}, u32[]{:S(2)}, u32[]{:S(2)}) async-start(bf16[4,64,2048]{2,1,0:T(8,128)(2,1)} %get-tuple-element.39), calls=%async_computation.1 | async-start | bytes 2097152 | tf_op jit(solution)/shard_map/all_to_all | solution.py:86
  65.4 6.9 %all-to-all-start.4 = ((bf16[4,64,2]{1,2,0:T(2,128)(2,1)}), bf16[4,64,2]{1,2,0:T(2,128)(2,1)S(1)}, u32[]{:S(2)}, u32[]{:S(2)}) async-start(bf16[4,64,2]{1,2,0:T(2,128)(2,1)} %copy.51), calls=%async_computation.4 | async-start | bytes 4096 | tf_op jit(solution)/shard_map/all_to_all | solution.py:127
  77.3 0.6 copy-start.8
  82.8 6.9 %all-to-all-start = ((bf16[4,64,2]{1,2,0:T(2,128)(2,1)}), bf16[4,64,2]{1,2,0:T(2,128)(2,1)S(1)}, u32[]{:S(2)}, u32[]{:S(2)}) async-start(bf16[4,64,2]{1,2,0:T(2,128)(2,1)} %copy.49), calls=%async_computation | async-start | bytes 4096 | tf_op jit(solution)/shard_map/all_to_all | solution.py:93
  86.0 265.2 %all-reduce.2.cloned.1.call-start = ((), (), s32[]{:S(2)}) async-start(), calls=%async_computation.7 | async-start | bytes 2097152 | tf_op jit(solution)/shard_map/psum | solution.py:156
  89.2 276.1 %reduce-scatter.5.cloned.1.call-start = ((), (), s32[]{:S(2)}) async-start(), calls=%async_computation.9 | async-start | bytes 7077888 | tf_op jit(solution)/shard_map/reduce_scatter | solution.py:163
  95.7 336.9 %reduce-scatter.3.cloned.1.call-start = ((), (), s32[]{:S(2)}) async-start(), calls=%async_computation.8 | async-start | bytes 14155776 | tf_op jit(solution)/shard_map/reduce_scatter | solution.py:160
  117.8 236.0 %copy-start.10 = (s32[1024]{0:T(1024)S(1)}, s32[1024]{0:T(1024)}, u32[]{:S(2)}) copy-start(s32[1024]{0:T(1024)} %copy-done.9) | copy-start | bytes 12292
  117.8 236.0 %all-to-all-start.3 = ((bf16[4,64,2048]{2,1,0:T(8,128)(2,1)}), bf16[4,64,2048]{2,1,0:T(8,128)(2,1)S(1)}, u32[]{:S(2)}, u32[]{:S(2)}) async-start(bf16[4,64,2048]{2,1,0:T(8,128)(2,1)} %bitcast.9), calls=%async_computation.3 | async-start | bytes 2097152 | tf_op jit(solution)/shard_map/all_to_all | solution.py:120
  356.3 2.3 copy-start.6
  356.3 76.3 %copy-start.1 = (bf16[128,2048]{1,0:T(8,128)(2,1)S(1)}, bf16[128,2048]{1,0:T(8,128)(2,1)}, u32[]{:S(2)}) copy-start(bf16[128,2048]{1,0:T(8,128)(2,1)} %param.7) | copy-start | bytes 1572868
  358.6 5.6 %copy-start.4 = (bf16[2048,128]{1,0:T(8,128)(2,1)S(1)}, bf16[2048,128]{1,0:T(8,128)(2,1)}, u32[]{:S(2)}) copy-start(bf16[2048,128]{1,0:T(8,128)(2,1)} %param.10) | copy-start | bytes 1572868
Sparse Core Ops, SparseCore 0:
  92.6 258.5 all-reduce.1
Sparse Core Ops, SparseCore 1:
  95.8 123.6 reduce-scatter.4
  223.5 209.1 reduce-scatter.2
where the time goes:
time: 441 us; the launch traced here: 440 us
  waiting for transfers between devices  316 us (72%)
  matrix products  43.3 us (10%)
  local copies, waits for them, and re-layouts  26.9 us (6%)
  other arithmetic  19.7 us (4%)
  starting transfers between devices  18.5 us (4%)
  between operations  15.8 us (4%)
    psum x1, waiting for transfers between devices, per_device(): router_grad = lax.psum(router_part, ('dp', 'expert'))  230 us
    reduce_scatter x1, waiting for transfers between devices, per_device(): lax.psum_scatter(part_gateup[None], 'dp', scatter_dimension=1, tiled=True)  67.3 us
    all_to_all x1, waiting for transfers between devices, per_device(): lax.all_to_all(send_in.reshape(flight, capacity, width), 'expert', split_...  13.1 us
    dot_general x1, matrix products, expert_rows(): pre_act = jnp.dot(rows_in, w_gateup, preferred_element_type=jnp.float32)  9.69 us
    dot_general x1, matrix products, expert_rows(): lax.dot_general(pre_grad, w_gateup, (((1,), (1,)), ((), ())), preferred_e...  9.05 us
  transfers between devices with their start and end apart: 8, of which 6 were waited for; matrix products, arithmetic and copies ran while one was open for 13% of the time, Pallas kernels for 0%

commit v1 on v0

--- a/solution.py
+++ b/solution.py
@@ -153,7 +153,11 @@
     router_part = lax.dot_general(
         tokens, logit_grad, (((0,), (0,)), ((), ())), preferred_element_type=jnp.float32
     )
-    router_grad = lax.psum(router_part, ("dp", "expert"))
+
+    def stacks_all_produce(body):
+        return lax.psum(lax.psum(body, "expert"), axis_name="dp")
+
+    router_grad = stacks_all_produce(router_part)
     part_gateup = acc_gateup.astype(jnp.bfloat16)
     part_down = acc_down.astype(jnp.bfloat16)
     gate_up_grad, down_grad = (

time: 441 us -> 539 us (1.22)
  waiting for transfers between devices: 316 us -> 404 us
  blocking collectives: 0 us -> 23 us
  starting transfers between devices: 18.5 us -> 11.5 us
    psum x1 -> x2, waiting for transfers between devices: 230 us -> 55.6 us  [stacks_all_produce(): return lax.psum(lax.psum(body, 'expert'), axis_name='dp')]
    reduce_scatter x1, waiting for transfers between devices: 67.3 us -> 211 us  [per_device(): lax.psum_scatter(part_gateup[None], 'dp', scatter_dimension=1, tiled=True)]
    reduce_scatter x1, waiting for transfers between devices: 0.01 us -> 119 us  [per_device(): lax.psum_scatter(part_down[None], 'dp', scatter_dimension=1, tiled=True)]
    all_to_all x0 -> x2, blocking collectives: none -> 23 us  [the longest x1 16.9 us: per_device(): lax.all_to_all(back_rows.reshape(sources, capacity, width), 'expert', spl...]
    all_to_all x2 -> x0, starting transfers between devices: 7.09 us -> none  [the longest x1 3.87 us: per_device(): lax.all_to_all(back_rows.reshape(sources, capacity, width), 'expert', spl...]
  transfers between devices with their start and end apart: 8 -> 7, of which waited for: 6 -> 7; matrix products, arithmetic and copies ran while one was open for 13% -> 11% of each run, Pallas kernels for 0% -> 0%
where the time goes in v1:
time: 539 us; the launch traced here: 538 us
  waiting for transfers between devices  404 us (75%)
  matrix products  42.4 us (8%)
  local copies, waits for them, and re-layouts  25.7 us (5%)
  blocking collectives  23 us (4%)
  other arithmetic  17.3 us (3%)
  between operations  14.1 us (3%)
  starting transfers between devices  11.5 us (2%)
    reduce_scatter x1, waiting for transfers between devices, per_device(): lax.psum_scatter(part_gateup[None], 'dp', scatter_dimension=1, tiled=True)  211 us
    reduce_scatter x1, waiting for transfers between devices, per_device(): lax.psum_scatter(part_down[None], 'dp', scatter_dimension=1, tiled=True)  119 us
    psum x2, waiting for transfers between devices, stacks_all_produce(): return lax.psum(lax.psum(body, 'expert'), axis_name='dp')  55.6 us
    all_to_all x1, blocking collectives, per_device(): lax.all_to_all(back_rows.reshape(sources, capacity, width), 'expert', spl...  16.9 us
    all_to_all x1, waiting for transfers between devices, per_device(): lax.all_to_all(send_in.reshape(flight, capacity, width), 'expert', split_...  13.1 us
  transfers between devices with their start and end apart: 7, of which 7 were waited for; matrix products, arithmetic and copies ran while one was open for 11% of the time, Pallas kernels for 0%

profile of v1, /device:TPU:0, one launch (start us, length us, event | category | flops | bytes accessed | tf_op | source)
XLA Modules:
  0.0 538.0 jit_solution(5868426447416874383)
XLA Ops:
  7.2 0.7 broadcast_compare_fusion
  7.9 0.7 broadcast_multiply_fusion
  8.6 0.8 copy.45
  9.4 0.1 eq.42
  9.5 0.1 eq.38
  9.6 0.1 copy.42
  9.8 0.6 copy-done.5
  10.4 0.1 lt.55
  10.5 0.1 copy.44
  10.6 0.1 mul.92
  10.7 1.2 reduce-window.6
  11.9 0.2 slice_reduce_fusion
  12.1 0.2 reduce-window.9
  12.5 2.4 scatter_custom_fusion.1
  14.9 2.4 scatter_custom_fusion
  17.5 0.6 pad_clamp_fusion.1
  18.1 1.4 gather_fusion.2
  19.5 1.4 gather_fusion.1
  20.8 1.5 broadcast_select_fusion
  22.4 4.4 all-to-all-start.2
  26.8 0.4 exponential_reduce_fusion
  27.1 0.1 copy.47
  27.3 0.2 select_reduce_fusion.1
  27.5 0.5 multiply_multiply_fusion
  28.1 13.1 %all-to-all-done.2 = bf16[4,64,2048]{2,1,0:T(8,128)(2,1)S(1)} async-done(((bf16[4,64,2048]{2,1,0:T(8,128)(2,1)}), bf16[4,64,2048]{2,1,0:T(8,128)(2,1)S(1)}, u32[]{:S(2)}, u32[]{:S(2)}) %all-to-all-start.2) | async-done | bytes 1048608 | tf_op jit(solution)/shard_map/all_to_all | solution.py:79
  41.2 3.5 all-to-all-start.1
  44.7 9.7 %fusion.2 = f32[256,3072]{1,0:T(8,128)} fusion(bf16[256,2048]{1,0:T(8,128)(2,1)S(1)} %bitcast.81, bf16[1,2048,3072]{2,1,0:T(8,128)(2,1)} %param.12), kind=kOutput, calls=%fused_computation.9 | convolution fusion | flops 3221225472 | bytes 16777216 | tf_op jit(solution)/shard_map/dot_general | solution.py:9
  54.4 2.3 multiply_convert_fusion.1
  56.7 2.4 all-to-all-done.1
  59.1 4.8 fusion.24
  64.0 0.6 copy.51
  64.6 3.2 all-to-all-start.4
  67.8 0.2 all-reduce.3.cloned.1.call-start
  68.0 0.5 exponential_reduce_fusion.1
  68.6 2.9 all-to-all-done.4
  71.6 3.5 gather_fusion.4
  75.1 0.1 gather.31
  75.3 0.7 multiply_reduce_fusion
  76.0 0.2 select_reduce_fusion
  76.2 0.7 copy.54
  76.9 0.9 add_convert_fusion
  77.8 1.3 convolution_bitcast_fusion
  79.1 0.1 copy.48
  79.2 0.1 div.31
  79.3 2.1 gather_fusion
  81.6 34.9 %all-reduce.3.cloned.1.call-done = f32[2048,128]{0,1:T(8,128)} async-done(((f32[2048,128]{0,1:T(8,128)}), f32[2048,128]{0,1:T(8,128)}) %all-reduce.3.cloned.1.call-update) | async-done | bytes 1048592 | tf_op jit(solution)/shard_map/psum | solution.py:158
  116.6 6.1 %all_to_all.25 = bf16[4,64,2]{1,2,0:T(2,128)(2,1)S(1)} all-to-all(bf16[4,64,2]{1,2,0:T(2,128)(2,1)S(1)} %copy.49), channel_id=1, replica_groups=mesh['dp'=8,'expert'=4] {'expert'}, dimensions={0} | all-to-all | bytes 2048 | tf_op jit(solution)/shard_map/all_to_all | solution.py:93
  122.8 0.5 broadcast.186
  123.3 0.7 fusion.38
  124.0 0.2 fusion.22
  124.3 4.4 fusion.4
  128.9 0.2 multiply_convert_fusion
  129.1 6.0 %multiply_convert_fusion.3 = (bf16[256,1536]{1,0:T(8,128)(2,1)S(1)}, bf16[256,1536]{1,0:T(8,128)(2,1)S(1)}) fusion(f32[256,3072]{1,0:T(8,128)} %fusion.2, bf16[256,2048]{1,0:T(8,128)(2,1)S(1)} %bitcast.85, bf16[1,1536,2048]{2,1,0:T(8,128)(2,1)} %param.13), kind=kOutput, calls=%fused_computation.32 | convolution fusion | flops 1615724544 | bytes 12058624 | tf_op jit(solution)/shard_map/dot_general | solution.py:15
  135.2 6.7 %convert_bitcast_fusion = bf16[1,2048,3072]{2,1,0:T(8,128)(2,1)} fusion(bf16[256,2048]{1,0:T(8,128)(2,1)S(1)} %bitcast.82, bf16[256,1536]{1,0:T(8,128)(2,1)S(1)} %get-tuple-element.31, bf16[256,1536]{1,0:T(8,128)(2,1)S(1)} %get-tuple-element.30), kind=kOutput, calls=%fused_computation.11 | convolution fusion | flops 3230662656 | bytes 15204352 | tf_op jit(solution)/shard_map/dot_general | solution.py:25
  141.8 8.0 %fusion.18 = bf16[256,2048]{1,0:T(8,128)(2,1)S(1)} fusion(bf16[1,2048,3072]{2,1,0:T(8,128)(2,1)} %param.12, bf16[256,1536]{1,0:T(8,128)(2,1)S(1)} %get-tuple-element.31, bf16[256,1536]{1,0:T(8,128)(2,1)S(1)} %get-tuple-element.30), kind=kOutput, calls=%fused_computation.22 | convolution fusion | flops 3224895488 | bytes 15204352 | tf_op jit(solution)/shard_map/dot_general | solution.py:28
  149.9 16.9 %all_to_all.26 = bf16[4,64,2048]{2,1,0:T(8,128)(2,1)S(1)} all-to-all(bf16[4,64,2048]{2,1,0:T(8,128)(2,1)S(1)} %bitcast.86), channel_id=1, replica_groups=mesh['dp'=8,'expert'=4] {'expert'}, dimensions={0} | all-to-all | bytes 2097152 | tf_op jit(solution)/shard_map/all_to_all | solution.py:120
  166.7 2.5 gather_fusion.3
  169.2 2.2 gather.29
  171.5 5.6 %convert_reduce_fusion = f32[128,2048]{1,0:T(8,128)S(1)} fusion(bf16[128,4,2048]{2,1,0:T(4,128)(2,1)} %gather.29, pred[128,4]{1,0:T(8,128)(4,1)S(1)} %copy-done.6), kind=kLoop, calls=%fused_computation.18 | loop fusion | flops 2883584 | bytes 3146240 | tf_op jit(solution)/shard_map/reduce_sum | solution.py:148
  177.1 1.1 fusion.21
  178.2 20.7 %all-reduce.5.cloned.1.call-done = f32[2048,128]{0,1:T(8,128)} async-done(((f32[2048,128]{0,1:T(8,128)}), f32[2048,128]{0,1:T(8,128)}) %all-reduce.5.cloned.1.call-update) | async-done | bytes 1048592 | tf_op jit(solution)/shard_map/psum | solution.py:158
  198.9 2.5 copy.55
  201.4 119.3 %reduce-scatter.5.cloned.1.call-done = bf16[1,192,2048]{2,1,0:T(8,128)(2,1)} async-done(((bf16[1,1536,2048]{2,1,0:T(8,128)(2,1)}), bf16[1,192,2048]{2,1,0:T(8,128)(2,1)}) %reduce-scatter.5.cloned.1.call-update) | async-done | bytes 786448 | tf_op jit(solution)/shard_map/reduce_scatter | solution.py:167
  320.7 210.8 %reduce-scatter.3.cloned.1.call-done = bf16[1,256,3072]{2,1,0:T(8,128)(2,1)} async-done(((bf16[1,2048,3072]{2,1,0:T(8,128)(2,1)}), bf16[1,256,3072]{2,1,0:T(8,128)(2,1)}) %reduce-scatter.3.cloned.1.call-update) | async-done | bytes 1572880 | tf_op jit(solution)/shard_map/reduce_scatter | solution.py:164
  (58 shorter events, 1.1 us)
Async XLA Ops:
  7.2 10.9 %copy-start = (bf16[128,2048]{1,0:T(8,128)(2,1)S(1)}, bf16[128,2048]{1,0:T(8,128)(2,1)}, u32[]{:S(2)}) copy-start(bf16[128,2048]{1,0:T(8,128)(2,1)} %param.7) | copy-start | bytes 1572868
  9.8 0.6 copy-start.5
  17.4 0.7 copy-start.10
  18.1 1.4 copy-start.2
  22.4 4.4 copy-start.3
  22.4 4.9 copy-start.7
  22.4 5.1 copy-start.12
  22.4 18.8 %all-to-all-start.2 = ((bf16[4,64,2048]{2,1,0:T(8,128)(2,1)}), bf16[4,64,2048]{2,1,0:T(8,128)(2,1)S(1)}, u32[]{:S(2)}, u32[]{:S(2)}) async-start(bf16[4,64,2048]{2,1,0:T(8,128)(2,1)} %get-tuple-element.38), calls=%async_computation.2 | async-start | bytes 2097152 | tf_op jit(solution)/shard_map/all_to_all | solution.py:79
  27.2 44.3 %copy-start.8 = (s32[1024]{0:T(1024)}, s32[1024]{0:T(1024)S(1)}, u32[]{:S(2)}) copy-start(s32[1024]{0:T(1024)S(1)} %pad_clamp_fusion) | copy-start | bytes 12292
  41.2 17.9 %all-to-all-start.1 = ((bf16[4,64,2048]{2,1,0:T(8,128)(2,1)}), bf16[4,64,2048]{2,1,0:T(8,128)(2,1)S(1)}, u32[]{:S(2)}, u32[]{:S(2)}) async-start(bf16[4,64,2048]{2,1,0:T(8,128)(2,1)} %get-tuple-element.39), calls=%async_computation.1 | async-start | bytes 2097152 | tf_op jit(solution)/shard_map/all_to_all | solution.py:86
  64.6 6.9 %all-to-all-start.4 = ((bf16[4,64,2]{1,2,0:T(2,128)(2,1)}), bf16[4,64,2]{1,2,0:T(2,128)(2,1)S(1)}, u32[]{:S(2)}, u32[]{:S(2)}) async-start(bf16[4,64,2]{1,2,0:T(2,128)(2,1)} %copy.51), calls=%async_computation.4 | async-start | bytes 4096 | tf_op jit(solution)/shard_map/all_to_all | solution.py:127
  67.8 48.7 %all-reduce.3.cloned.1.call-start = ((), (), s32[]{:S(2)}) async-start(), calls=%async_computation.7 | async-start | bytes 2097152 | tf_op jit(solution)/shard_map/psum | solution.py:158
  76.0 5.5 %copy-start.11 = (pred[256]{0:T(512)(128)(4,1)S(1)}, pred[256]{0:T(512)(128)(4,1)}, u32[]{:S(2)}) copy-start(pred[256]{0:T(512)(128)(4,1)} %copy-done.10) | copy-start | bytes 772
  79.1 119.8 %all-reduce.5.cloned.1.call-start = ((), (), s32[]{:S(2)}) async-start(), calls=%async_computation.8 | async-start | bytes 2097152 | tf_op jit(solution)/shard_map/psum | solution.py:158
  116.6 204.2 %reduce-scatter.5.cloned.1.call-start = ((), (), s32[]{:S(2)}) async-start(), calls=%async_computation.10 | async-start | bytes 7077888 | tf_op jit(solution)/shard_map/reduce_scatter | solution.py:167
  128.7 402.7 %reduce-scatter.3.cloned.1.call-start = ((), (), s32[]{:S(2)}) async-start(), calls=%async_computation.9 | async-start | bytes 14155776 | tf_op jit(solution)/shard_map/reduce_scatter | solution.py:164
  149.9 16.9 %copy-start.9 = (s32[1024]{0:T(1024)S(1)}, s32[1024]{0:T(1024)}, u32[]{:S(2)}) copy-start(s32[1024]{0:T(1024)} %copy-done.8) | copy-start | bytes 12292
  169.2 2.3 copy-start.6
  171.5 5.6 %copy-start.4 = (bf16[2048,128]{1,0:T(8,128)(2,1)S(1)}, bf16[2048,128]{1,0:T(8,128)(2,1)}, u32[]{:S(2)}) copy-start(bf16[2048,128]{1,0:T(8,128)(2,1)} %param.10) | copy-start | bytes 1572868
  171.5 360.0 %copy-start.1 = (bf16[128,2048]{1,0:T(8,128)(2,1)S(1)}, bf16[128,2048]{1,0:T(8,128)(2,1)}, u32[]{:S(2)}) copy-start(bf16[128,2048]{1,0:T(8,128)(2,1)} %param.7) | copy-start | bytes 1572868
Sparse Core Ops, SparseCore 0:
  79.2 37.2 all-reduce.2
  120.0 78.8 all-reduce.4
  203.1 117.6 reduce-scatter.4
  324.7 206.7 reduce-scatter.2
